TPU v7x, 16 devices: a 4x2x1 block of a 4x4x8 slice. The times are simulated.
16 devices in a mesh: data: 2 (over y, z), tp: 8 (over x, core).
Axes of the slice: x: 4, y: 2, z: 1, core: 2. Of those that a mesh axis runs over, the one named last changes fastest.
The devices are a block of a 4x4x8 slice.
Arguments:
- attn_out: bfloat16 [1024, 12288], P('data', 'tp'), parts along dimension 0
- w_out: bfloat16 [12288, 12288], P('tp')
- residual: bfloat16 [1024, 12288], P('data', 'tp'), parts along dimension 0
- norm_gain: float32 [12288], P('tp')
Outputs:
- output 1: bfloat16 [1024, 12288], P('data', 'tp'), parts along dimension 0
- output 2: bfloat16 [1024, 12288], P('data', 'tp'), parts along dimension 0
There are 2 independent parts. A program takes and returns all parts, laid end to end along the dimension named above; an argument that names none is the same for every part.
All inputs are finite; a program needn't handle non-finite values.
Results may differ from a plain program's by a relative error of at most 0.00634263.
Values are sent between devices in bfloat16 or wider.
A program may use at most 768 MiB of HBM per device.

v0:
```python
import jax
import jax.numpy as jnp
from jax import lax
from jax.sharding import PartitionSpec as P, NamedSharding

EPS = 1e-5


def solution(mesh):
    tp_size = mesh.shape["tp"]

    def local_step(attn_blk, w_blk, resid_blk, gain_blk):
        tok_rows = attn_blk.shape[0]
        d_local = resid_blk.shape[1]
        d_model = d_local * tp_size
        partial = jnp.dot(attn_blk, w_blk, preferred_element_type=jnp.float32).astype(jnp.bfloat16)
        received = lax.all_to_all(partial, "tp", 1, 0, tiled=True)
        projected = jnp.sum(received.reshape(tp_size, tok_rows, d_local), axis=0, dtype=jnp.float32)
        hidden = resid_blk.astype(jnp.float32) + projected
        sq_part = jnp.sum(hidden * hidden, axis=-1, keepdims=True)
        sq_total = lax.psum(sq_part, "tp")
        normed = hidden * lax.rsqrt(sq_total / d_model + EPS) * gain_blk
        return hidden.astype(jnp.bfloat16), normed.astype(jnp.bfloat16)

    return jax.shard_map(
        local_step,
        mesh=mesh,
        in_specs=(P("data", "tp"), P("tp", None), P("data", "tp"), P("tp")),
        out_specs=(P("data", "tp"), P("data", "tp")),
        check_vma=False,
    )
```

profile of v0, /device:TPU:113, one launch (start us, length us, event | category | flops | bytes accessed | tf_op | source)
XLA Modules:
  0.0 207.5 jit_solution(4316457929401678031)
XLA Ops:
  0.6 0.0 copy-start
  0.6 1.4 copy-done
  2.0 26.7 %convolution_convert_fusion = bf16[512,12288]{1,0:T(8,128)(2,1)} fusion(bf16[512,1536]{1,0:T(8,128)(2,1)S(1)} %copy-done, bf16[1536,12288]{1,0:T(8,128)(2,1)} %param.5), kind=kOutput, calls=%fused_computation.1 | convolution fusion | flops 19333644288 | bytes 51904512 | tf_op jit(solution)/shard_map/dot_general | solution.py:16
  28.7 6.4 %copy.9 = bf16[64,8,8,1536]{3,2,0,1:T(8,128)(2,1)S(1)} copy(bf16[64,8,8,1536]{3,2,1,0:T(8,128)(2,1)} %bitcast.9) | data formatting | bytes 25165824 | tf_op jit(solution)/shard_map/all_to_all | solution.py:17
  35.1 144.4 %all_to_all.13 = bf16[512,8,1536]{2,0,1:T(8,128)(2,1)} all-to-all(bf16[512,8,1536]{2,0,1:T(8,128)(2,1)S(1)} %bitcast.8), channel_id=1, replica_groups=mesh['data'=2,'tp'=8] {'tp'}, dimensions={1} | all-to-all | bytes 25165824 | tf_op jit(solution)/shard_map/all_to_all | solution.py:17
  179.5 0.0 copy-start.2
  179.5 8.4 %convert_reduce_fusion = f32[512,1536]{1,0:T(8,128)} fusion(bf16[512,8,1536]{2,0,1:T(8,128)(2,1)} %all_to_all.13), kind=kLoop, calls=%fused_computation | loop fusion | flops 11796480 | bytes 15728640 | tf_op jit(solution)/shard_map/reduce_sum | solution.py:18
  188.0 0.0 copy-done.2
  188.0 0.0 copy-start.3
  188.0 2.4 %multiply_reduce_fusion = f32[512]{0:T(512)S(1)} fusion(f32[512,1536]{1,0:T(8,128)} %convert_reduce_fusion, bf16[512,1536]{1,0:T(8,128)(2,1)S(1)} %copy-done.2), kind=kLoop, calls=%fused_computation.4 | loop fusion | flops 3145216 | bytes 4720640 | tf_op jit(solution)/shard_map/reduce_sum | solution.py:20
  190.4 12.9 %psum.7 = f32[512,1]{0,1:T(1,128)S(1)} all-reduce(f32[512,1]{0,1:T(1,128)S(1)} %bitcast.11), channel_id=1, replica_groups=mesh['data'=2,'tp'=8] {'tp'}, use_global_device_ids=true, to_apply=%region_2.0 | all-reduce | flops 512 | bytes 4096 | tf_op jit(solution)/shard_map/psum | solution.py:21
  203.3 0.0 copy-start.1
  203.3 0.0 copy-done.3
  203.3 4.2 %multiply_convert_fusion = (bf16[512,1536]{1,0:T(8,128)(2,1)}, bf16[512,1536]{1,0:T(8,128)(2,1)}) fusion(f32[1536]{0:T(1024)S(1)} %copy-done.3, f32[512]{0:T(512)S(1)} %bitcast.10, f32[512,1536]{1,0:T(8,128)} %convert_reduce_fusion, bf16[512,1536]{1,0:T(8,128)(2,1)S(1)} %copy-done.2), kind=kLoop, calls=%fused_computation.3 | loop fusion | flops 4718592 | bytes 7872512 | tf_op jit(solution)/shard_map/convert_element_type | solution.py:23
  207.5 0.0 copy-done.1
  (1 shorter events, 0.0 us)
Async XLA Ops:
  0.6 1.4 copy-start
  179.5 8.4 %copy-start.2 = (bf16[512,1536]{1,0:T(8,128)(2,1)S(1)}, bf16[512,1536]{1,0:T(8,128)(2,1)}, u32[]{:S(2)}) copy-start(bf16[512,1536]{1,0:T(8,128)(2,1)} %param.6) | copy-start | bytes 4718596
  188.0 15.3 %copy-start.3 = (f32[1536]{0:T(1024)S(1)}, f32[1536]{0:T(1024)}, u32[]{:S(2)}) copy-start(f32[1536]{0:T(1024)} %param.7) | copy-start | bytes 18436
  203.3 4.2 %copy-start.1 = (bf16[512,1536]{1,0:T(8,128)(2,1)S(1)}, bf16[512,1536]{1,0:T(8,128)(2,1)}, u32[]{:S(2)}) copy-start(bf16[512,1536]{1,0:T(8,128)(2,1)} %param.4) | copy-start | bytes 4718596
where the time goes:
time: 208 us; the launch traced here: 207 us
  blocking collectives  157 us (75%)
  matrix products  26.7 us (13%)
  other arithmetic  15 us (7%)
  local copies, waits for them, and re-layouts  7.84 us (4%)
    all_to_all x1, blocking collectives, local_step(): received = lax.all_to_all(partial, 'tp', 1, 0, tiled=True)  144 us
    dot_general x1, matrix products, local_step(): jnp.dot(attn_blk, w_blk, preferred_element_type=jnp.float32)  26.7 us
    psum x1, blocking collectives, local_step(): sq_total = lax.psum(sq_part, 'tp')  12.9 us
    reduce_sum x1, other arithmetic, local_step(): jnp.sum(received.reshape(tp_size, tok_rows, d_local), axis=0, dtype=jnp.f...  8.44 us
    all_to_all x1, local copies, waits for them, and re-layouts, local_step(): received = lax.all_to_all(partial, 'tp', 1, 0, tiled=True)  6.42 us
    convert_element_type x1, other arithmetic, local_step(): return (hidden.astype(jnp.bfloat16), normed.astype(jnp.bfloat16))  4.19 us

commit v1 on v0

v1 whole, which is shorter than its diff:
```python
import functools

import jax
import jax.numpy as jnp
from jax import lax
from jax.experimental import pallas as pl
from jax.experimental.pallas import tpu as pltpu
from jax.sharding import PartitionSpec as P

EPS = 1e-5
MESH = pl.DeviceIdType.MESH
CORES = 2
CHIPS = 4
UNIT = 256
W_SLOTS = 4
RB = 64
AHEAD = 3
LAG = 3


def _kernel(
    tp_size, d_model,
    a_hbm, w_hbm, r_hbm, g_hbm, hid_hbm, nrm_hbm,
    a, w, p, rx, relay_out, relay_in, res, gain, hbuf, hout, nout, sq_out, sq_in,
    in_sem, w_sem, send_sem, recv_sem, rsend_sem, rrecv_sem, qsend_sem, qrecv_sem, out_sem,
):
    rows, d_local = r_hbm.shape
    half = d_local // 2
    nu = half // UNIT
    per_group = CORES * 2 * nu
    total = CHIPS * per_group
    chunks = rows // RB

    me = lax.axis_index("tp")
    x, c = lax.div(me, CORES), lax.rem(me, CORES)

    def chip(offset, core):
        return lax.rem(x + offset, CHIPS) * CORES + core

    def decode(s):
        g, j = lax.div(s, per_group), lax.rem(s, per_group)
        i, eb, hh = lax.div(j, 4), lax.rem(lax.div(j, 2), 2), lax.rem(j, 2)
        return g, i, eb, lax.rem(eb + 1 + c, 2), lax.rem(hh + c, 2)

    def w_copy(s):
        g, i, _, e, h = decode(s)
        o = lax.rem(6 - g + 2 * h * lax.rem(g, 2), CHIPS)
        col = pl.multiple_of(chip(o, e) * d_local + h * half + i * UNIT, UNIT)
        k = lax.rem(s, W_SLOTS)
        return pltpu.make_async_copy(w_hbm.at[:, pl.ds(col, UNIT)], w.at[k], w_sem.at[k])

    def block_copy(s, slot, target):
        return pltpu.make_async_remote_copy(
            src_ref=p.at[s], dst_ref=rx.at[slot], send_sem=send_sem.at[s], recv_sem=recv_sem.at[slot],
            device_id={"tp": target}, device_id_type=MESH)

    def local_unit(g, h, i):
        return g * per_group + i * 4 + 2 + lax.rem(h + c, 2)

    def relay_copy(h, r):
        return pltpu.make_async_remote_copy(
            src_ref=relay_out.at[h, r], dst_ref=relay_in.at[h, r],
            send_sem=rsend_sem.at[h, r], recv_sem=rrecv_sem.at[h, r],
            device_id={"tp": chip(3 - 2 * h, c)}, device_id_type=MESH)

    def sq_copy(r, t):
        return pltpu.make_async_remote_copy(
            src_ref=sq_out.at[r], dst_ref=sq_in.at[r, me],
            send_sem=qsend_sem.at[r, t], recv_sem=qrecv_sem.at[r, me],
            device_id={"tp": lax.rem(me + t, tp_size)}, device_id_type=MESH)

    def chunk_rows(r):
        return pl.ds(pl.multiple_of(r * RB, RB), RB)

    barrier = pltpu.get_barrier_semaphore()
    for t in range(1, tp_size):
        pl.semaphore_signal(barrier, inc=1, device_id={"tp": lax.rem(me + t, tp_size)}, device_id_type=MESH)

    w_copy(jnp.int32(0)).start()
    a_copy = pltpu.make_async_copy(a_hbm, a, in_sem.at[0])
    a_copy.start()
    for s in range(1, W_SLOTS):
        w_copy(jnp.int32(s)).start()
    r_copy = pltpu.make_async_copy(r_hbm, res, in_sem.at[1])
    r_copy.start()
    g_copy = pltpu.make_async_copy(g_hbm, gain, in_sem.at[2])
    g_copy.start()
    a_copy.wait()

    @pl.loop(0, total)
    def _(s):
        g, i, eb, e, h = decode(s)
        w_copy(s).wait()
        k = lax.rem(s, W_SLOTS)
        p[s] = jnp.dot(a[...], w[k], preferred_element_type=jnp.float32).astype(p.dtype)

        @pl.when(s + W_SLOTS < total)
        def _():
            w_copy(s + W_SLOTS).start()

        @pl.when(s == 0)
        def _():
            pl.semaphore_wait(barrier, tp_size - 1)

        @pl.when(g == 0)
        def _():
            block_copy(s, (h * 2 + c) * nu + i, chip(3 + 2 * h, e)).start()

        @pl.when(g == 1)
        def _():
            block_copy(s, (4 + h * 2 + c) * nu + i, chip(1 + 2 * h, e)).start()

        @pl.when(jnp.logical_and(g >= 2, eb == 0))
        def _():
            block_copy(s, (4 + g * 2 + h) * nu + i, x * CORES + 1 - c).start()

    def wait_blocks(lo, hi):
        @pl.loop(lo, hi)
        def _(slot):
            block_copy(0, slot, me).wait_recv()

    wait_blocks(0, 4 * nu)
    wait_blocks(10 * nu, 12 * nu)

    @pl.loop(0, chunks)
    def _(r):
        rs = chunk_rows(r)
        for h in range(2):
            for i in range(nu):
                acc = p[local_unit(3, h, i), rs, :].astype(jnp.float32)
                acc += rx[(10 + h) * nu + i, rs, :].astype(jnp.float32)
                acc += rx[(h * 2) * nu + i, rs, :].astype(jnp.float32)
                acc += rx[(h * 2 + 1) * nu + i, rs, :].astype(jnp.float32)
                relay_out[h, r, :, i * UNIT:(i + 1) * UNIT] = acc

        @pl.when(r < AHEAD)
        def _():
            for h in range(2):
                relay_copy(h, r).start()

    r_copy.wait()
    g_copy.wait()
    wait_blocks(8 * nu, 10 * nu)
    wait_blocks(4 * nu, 8 * nu)

    eye = (lax.broadcasted_iota(jnp.int32, (RB, 128), 0)
           == lax.broadcasted_iota(jnp.int32, (RB, 128), 1))

    def hid_copy(r):
        return pltpu.make_async_copy(hout.at[r], hid_hbm.at[chunk_rows(r), :], out_sem.at[0, r])

    def nrm_copy(r):
        return pltpu.make_async_copy(nout.at[r], nrm_hbm.at[chunk_rows(r), :], out_sem.at[1, r])

    def normalise(r):
        for t in range(1, tp_size):
            src = lax.rem(me + t, tp_size)
            pltpu.make_async_remote_copy(
                src_ref=sq_out.at[r], dst_ref=sq_in.at[r, src],
                send_sem=qsend_sem.at[r, t], recv_sem=qrecv_sem.at[r, src],
                device_id={"tp": src}, device_id_type=MESH).wait_recv()
        tot = sq_in[r, 0]
        for t in range(1, tp_size):
            tot += sq_in[r, t]
        col = jnp.sum(jnp.where(eye, jnp.broadcast_to(tot, (RB, 128)), 0.0), axis=1, keepdims=True)
        scale = lax.rsqrt(col / d_model + EPS)
        nout[r] = (hbuf[r] * scale * gain[...]).astype(nout.dtype)
        nrm_copy(r).start()

    @pl.loop(0, chunks)
    def _(r):
        @pl.when(r + AHEAD < chunks)
        def _():
            for h in range(2):
                relay_copy(h, r + AHEAD).start()

        rs = chunk_rows(r)
        sq = jnp.zeros((RB, UNIT), jnp.float32)
        for h in range(2):
            relay_copy(h, r).wait_recv()
            for i in range(nu):
                cols = slice(h * half + i * UNIT, h * half + (i + 1) * UNIT)
                acc = p[local_unit(2, h, i), rs, :].astype(jnp.float32)
                acc += rx[(8 + h) * nu + i, rs, :].astype(jnp.float32)
                acc += rx[(4 + h * 2) * nu + i, rs, :].astype(jnp.float32)
                acc += rx[(5 + h * 2) * nu + i, rs, :].astype(jnp.float32)
                acc += relay_in[h, r, :, i * UNIT:(i + 1) * UNIT]
                acc += res[rs, cols].astype(jnp.float32)
                hbuf[r, :, cols] = acc
                hout[r, :, cols] = acc.astype(hout.dtype)
                sq += acc * acc
        sq = jnp.sum(sq, axis=1, keepdims=True)
        packed = jnp.sum(jnp.where(eye, jnp.broadcast_to(sq, (RB, 128)), 0.0), axis=0, keepdims=True)
        sq_out[r] = packed
        sq_in[r, me] = packed
        hid_copy(r).start()
        for t in range(1, tp_size):
            sq_copy(r, t).start()

        @pl.when(r >= LAG)
        def _():
            normalise(r - LAG)

    @pl.loop(chunks - LAG, chunks)
    def _(r):
        normalise(r)

    @pl.loop(0, total)
    def _(s):
        g, i, eb, e, h = decode(s)

        @pl.when(jnp.logical_or(g < 2, eb == 0))
        def _():
            block_copy(s, 0, me).wait_send()

    @pl.loop(0, chunks)
    def _(r):
        for h in range(2):
            relay_copy(h, r).wait_send()
        for t in range(1, tp_size):
            sq_copy(r, t).wait_send()
        hid_copy(r).wait()
        nrm_copy(r).wait()


def solution(mesh):
    tp_size = mesh.shape["tp"]

    def local_step(attn_blk, w_blk, resid_blk, gain_blk):
        rows, k_dim = attn_blk.shape
        d_local = resid_blk.shape[1]
        d_model = w_blk.shape[1]
        half = d_local // 2
        nu = half // UNIT
        units = tp_size * 2 * nu
        chunks = rows // RB
        assert tp_size == CORES * CHIPS and half % UNIT == 0 and rows % RB == 0
        any_spec = pl.BlockSpec(memory_space=pl.ANY)
        dma = pltpu.SemaphoreType.DMA
        return pl.pallas_call(
            functools.partial(_kernel, tp_size, d_model),
            out_shape=[jax.ShapeDtypeStruct((rows, d_local), jnp.bfloat16)] * 2,
            in_specs=[any_spec] * 4,
            out_specs=[any_spec] * 2,
            scratch_shapes=[
                pltpu.VMEM((rows, k_dim), jnp.bfloat16),
                pltpu.VMEM((W_SLOTS, k_dim, UNIT), jnp.bfloat16),
                pltpu.VMEM((units, rows, UNIT), jnp.bfloat16),
                pltpu.VMEM((12 * nu, rows, UNIT), jnp.bfloat16),
                pltpu.VMEM((2, chunks, RB, half), jnp.float32),
                pltpu.VMEM((2, chunks, RB, half), jnp.float32),
                pltpu.VMEM((rows, d_local), jnp.bfloat16),
                pltpu.VMEM((1, d_local), jnp.float32),
                pltpu.VMEM((chunks, RB, d_local), jnp.float32),
                pltpu.VMEM((chunks, RB, d_local), jnp.bfloat16),
                pltpu.VMEM((chunks, RB, d_local), jnp.bfloat16),
                pltpu.VMEM((chunks, 1, 128), jnp.float32),
                pltpu.VMEM((chunks, tp_size, 1, 128), jnp.float32),
                dma((3,)),
                dma((W_SLOTS,)),
                dma((units,)),
                dma((12 * nu,)),
                dma((2, chunks)),
                dma((2, chunks)),
                dma((chunks, tp_size)),
                dma((chunks, tp_size)),
                dma((2, chunks)),
            ],
            compiler_params=pltpu.CompilerParams(
                collective_id=0, has_side_effects=True, vmem_limit_bytes=56 * 1024 * 1024
            ),
            name="proj_scatter_norm",
        )(attn_blk, w_blk, resid_blk, gain_blk.reshape(1, d_local))

    return jax.shard_map(
        local_step,
        mesh=mesh,
        in_specs=(P("data", "tp"), P("tp", None), P("data", "tp"), P("tp")),
        out_specs=(P("data", "tp"), P("data", "tp")),
        check_vma=False,
    )
```

time: 208 us -> 122 us (0.59)
  blocking collectives: 157 us -> 0 us
  Pallas kernels: 0 us -> 116 us
  matrix products: 26.7 us -> 0 us
  other arithmetic: 15 us -> 0 us
  local copies, waits for them, and re-layouts: 7.84 us -> 5.21 us
    all_to_all x1 -> x0, blocking collectives: 144 us -> none  [local_step(): received = lax.all_to_all(partial, 'tp', 1, 0, tiled=True)]
    pallas_call x0 -> x1, Pallas kernels: none -> 116 us  [local_step(): pl.pallas_call(functools.partial(_kernel, tp_size, d_model), out_shape=[j...]
    dot_general x1 -> x0, matrix products: 26.7 us -> none  [local_step(): jnp.dot(attn_blk, w_blk, preferred_element_type=jnp.float32)]
    psum x1 -> x0, blocking collectives: 12.9 us -> none  [local_step(): sq_total = lax.psum(sq_part, 'tp')]
    reduce_sum x2 -> x0, other arithmetic: 10.8 us -> none  [the longest x1 8.44 us: local_step(): jnp.sum(received.reshape(tp_size, tok_rows, d_local), axis=0, dtype=jnp.f...]
    all_to_all x1 -> x0, local copies, waits for them, and re-layouts: 6.42 us -> none  [local_step(): received = lax.all_to_all(partial, 'tp', 1, 0, tiled=True)]
    convert_element_type x1 -> x0, other arithmetic: 4.19 us -> none  [local_step(): return (hidden.astype(jnp.bfloat16), normed.astype(jnp.bfloat16))]
    unnamed x8 -> x4, local copies, waits for them, and re-layouts: 1.42 us -> 3.92 us
where the time goes in v1:
time: 122 us
  Pallas kernels  116 us (95%)
  local copies, waits for them, and re-layouts  5.21 us (4%)
    pallas_call x1, Pallas kernels, local_step(): pl.pallas_call(functools.partial(_kernel, tp_size, d_model), out_shape=[j...  116 us
    unnamed x4, local copies, waits for them, and re-layouts  3.92 us

profile of v1, /device:TPU:113, one launch (start us, length us, event | category | flops | bytes accessed | tf_op | source)
XLA Modules:
  0.0 122.1 jit_solution(648036850571237384)
XLA Ops:
  0.6 1.3 %reshape.7.g_hbm = f32[1,1536]{1,0:T(1,128)} reshape(f32[1536]{0:T(1024)} %param.7) | data formatting | bytes 12288 | tf_op jit(solution)/shard_map/reshape | solution.py:273
  1.9 116.2 %proj_scatter_norm.1 = (bf16[512,1536]{1,0:T(8,128)(2,1)}, bf16[512,1536]{1,0:T(8,128)(2,1)}) custom-call(bf16[512,1536]{1,0:T(8,128)(2,1)} %a_hbm.1, bf16[1536,12288]{1,0:T(8,128)(2,1)} %w_hbm.1, bf16[512,1536]{1,0:T(8,128)(2,1)} %r_hbm.1, f32[1,1536]{1,0:T(1,128)} %reshape.7.g_hbm), custom_call_target="tpu_custom_call" | custom-call | tf_op jit(solution)/shard_map/proj_scatter_norm/pallas_call | solution.py:240
  118.2 0.0 copy-start
  118.2 2.8 %copy.8 = bf16[512,1536]{1,0:T(8,128)(2,1)} copy(bf16[512,1536]{1,0:T(8,128)(2,1)} %get-tuple-element.4) | data formatting | bytes 3145728
  120.9 0.0 copy-done
  120.9 1.1 copy.9
Async XLA Ops:
  118.2 2.8 %copy-start = (bf16[512,1536]{1,0:T(8,128)(2,1)S(1)}, bf16[512,1536]{1,0:T(8,128)(2,1)}, u32[]{:S(2)}) copy-start(bf16[512,1536]{1,0:T(8,128)(2,1)} %get-tuple-element.5) | copy-start | bytes 4718596

commit v2 on v1

v2 whole, which is shorter than its diff:
```python
import functools

import jax
import jax.numpy as jnp
from jax import lax
from jax.experimental import pallas as pl
from jax.experimental.pallas import tpu as pltpu
from jax.sharding import PartitionSpec as P

EPS = 1e-5
MESH = pl.DeviceIdType.MESH
CORES = 2
CHIPS = 4
UNIT = 256
W_SLOTS = 4
RB = 64
AHEAD = 3
LAG = 3
A_BLOCKS = 4


def _kernel(
    tp_size, d_model,
    a_hbm, w_hbm, r_hbm, g_hbm, hid, nrm,
    a, w, p, rx, relay_out, relay_in, res, gain, hbuf, sq_out, sq_in,
    a_sem, in_sem, w_sem, send_sem, recv_sem, rsend_sem, rrecv_sem, qsend_sem, qrecv_sem,
):
    rows, d_local = r_hbm.shape
    half = d_local // 2
    nu = half // UNIT
    per_group = CORES * 2 * nu
    total = CHIPS * per_group
    chunks = rows // RB
    ab = rows // A_BLOCKS

    me = lax.axis_index("tp")
    x, c = lax.div(me, CORES), lax.rem(me, CORES)

    def chip(offset, core):
        return lax.rem(x + offset, CHIPS) * CORES + core

    def decode(s):
        g, j = lax.div(s, per_group), lax.rem(s, per_group)
        i, eb, hh = lax.div(j, 4), lax.rem(lax.div(j, 2), 2), lax.rem(j, 2)
        return g, i, eb, lax.rem(eb + 1 + c, 2), lax.rem(hh + c, 2)

    def w_copy(s):
        g, i, _, e, h = decode(s)
        o = lax.rem(6 - g + 2 * h * lax.rem(g, 2), CHIPS)
        col = pl.multiple_of(chip(o, e) * d_local + h * half + i * UNIT, UNIT)
        k = lax.rem(s, W_SLOTS)
        return pltpu.make_async_copy(w_hbm.at[:, pl.ds(col, UNIT)], w.at[k], w_sem.at[k])

    def a_copy(b):
        rs = pl.ds(b * ab, ab)
        return pltpu.make_async_copy(a_hbm.at[rs, :], a.at[rs, :], a_sem.at[b])

    def send_rows(s, slot, group, target, rs):
        pltpu.make_async_remote_copy(
            src_ref=p.at[s, rs], dst_ref=rx.at[slot, rs], send_sem=send_sem.at[0], recv_sem=recv_sem.at[group],
            device_id={"tp": target}, device_id_type=MESH).start()

    def send_block(s, slot, group, target):
        send_rows(s, slot, group, target, pl.ds(0, rows))

    def wait_bytes(ref, sem):
        pltpu.make_async_copy(ref, ref, sem).wait()

    def local_unit(g, h, i):
        return g * per_group + i * 4 + 2 + lax.rem(h + c, 2)

    def send_relay(r):
        for h in range(2):
            pltpu.make_async_remote_copy(
                src_ref=relay_out.at[r, h], dst_ref=relay_in.at[r, h],
                send_sem=rsend_sem.at[0], recv_sem=rrecv_sem.at[r],
                device_id={"tp": chip(3 - 2 * h, c)}, device_id_type=MESH).start()

    def chunk_rows(r):
        return pl.ds(pl.multiple_of(r * RB, RB), RB)

    barrier = pltpu.get_barrier_semaphore()
    for t in range(1, tp_size):
        pl.semaphore_signal(barrier, inc=1, device_id={"tp": lax.rem(me + t, tp_size)}, device_id_type=MESH)

    w_copy(jnp.int32(0)).start()
    for b in range(A_BLOCKS):
        a_copy(b).start()
    for s in range(1, W_SLOTS):
        w_copy(jnp.int32(s)).start()
    r_copy = pltpu.make_async_copy(r_hbm, res, in_sem.at[0])
    r_copy.start()
    g_copy = pltpu.make_async_copy(g_hbm, gain, in_sem.at[1])
    g_copy.start()

    _, i0, _, e0, h0 = decode(jnp.int32(0))
    w_copy(jnp.int32(0)).wait()
    for b in range(A_BLOCKS):
        a_copy(b).wait()
        rs = pl.ds(b * ab, ab)
        p[0, rs, :] = jnp.dot(a[rs, :], w[0], preferred_element_type=jnp.float32).astype(p.dtype)
        if b == 0:
            pl.semaphore_wait(barrier, tp_size - 1)
        send_rows(0, (h0 * 2 + c) * nu + i0, 0, chip(3 + 2 * h0, e0), rs)
    w_copy(jnp.int32(W_SLOTS)).start()

    @pl.loop(1, total)
    def _(s):
        g, i, eb, e, h = decode(s)
        w_copy(s).wait()
        k = lax.rem(s, W_SLOTS)
        p[s] = jnp.dot(a[...], w[k], preferred_element_type=jnp.float32).astype(p.dtype)

        @pl.when(s + W_SLOTS < total)
        def _():
            w_copy(s + W_SLOTS).start()

        @pl.when(g == 0)
        def _():
            send_block(s, (h * 2 + c) * nu + i, 0, chip(3 + 2 * h, e))

        @pl.when(g == 1)
        def _():
            send_block(s, (4 + h * 2 + c) * nu + i, 1, chip(1 + 2 * h, e))

        @pl.when(jnp.logical_and(g >= 2, eb == 0))
        def _():
            send_block(s, (4 + g * 2 + h) * nu + i, g, x * CORES + 1 - c)

    wait_bytes(rx.at[pl.ds(0, 4 * nu)], recv_sem.at[0])
    wait_bytes(rx.at[pl.ds(10 * nu, 2 * nu)], recv_sem.at[3])

    @pl.loop(0, chunks)
    def _(r):
        rs = chunk_rows(r)
        for h in range(2):
            for i in range(nu):
                acc = p[local_unit(3, h, i), rs, :].astype(jnp.float32)
                acc += rx[(10 + h) * nu + i, rs, :].astype(jnp.float32)
                acc += rx[(h * 2) * nu + i, rs, :].astype(jnp.float32)
                acc += rx[(h * 2 + 1) * nu + i, rs, :].astype(jnp.float32)
                relay_out[r, h, :, i * UNIT:(i + 1) * UNIT] = acc

        @pl.when(r < AHEAD)
        def _():
            send_relay(r)

    r_copy.wait()
    g_copy.wait()
    wait_bytes(rx.at[pl.ds(8 * nu, 2 * nu)], recv_sem.at[2])
    wait_bytes(rx.at[pl.ds(4 * nu, 4 * nu)], recv_sem.at[1])

    eye = (lax.broadcasted_iota(jnp.int32, (RB, 128), 0)
           == lax.broadcasted_iota(jnp.int32, (RB, 128), 1))

    def normalise(r):
        wait_bytes(sq_in.at[r, pl.ds(0, tp_size - 1)], qrecv_sem.at[r])
        tot = sq_in[r, 0]
        for t in range(1, tp_size):
            tot += sq_in[r, t]
        col = jnp.sum(jnp.where(eye, jnp.broadcast_to(tot, (RB, 128)), 0.0), axis=1, keepdims=True)
        scale = lax.rsqrt(col / d_model + EPS)
        nrm[chunk_rows(r), :] = (hbuf[r] * scale * gain[...].reshape(1, d_local)).astype(nrm.dtype)

    @pl.loop(0, chunks)
    def _(r):
        @pl.when(r + AHEAD < chunks)
        def _():
            send_relay(r + AHEAD)

        wait_bytes(relay_in.at[r], rrecv_sem.at[r])
        rs = chunk_rows(r)
        sq = jnp.zeros((RB, UNIT), jnp.float32)
        for h in range(2):
            for i in range(nu):
                cols = slice(h * half + i * UNIT, h * half + (i + 1) * UNIT)
                acc = p[local_unit(2, h, i), rs, :].astype(jnp.float32)
                acc += rx[(8 + h) * nu + i, rs, :].astype(jnp.float32)
                acc += rx[(4 + h * 2) * nu + i, rs, :].astype(jnp.float32)
                acc += rx[(5 + h * 2) * nu + i, rs, :].astype(jnp.float32)
                acc += relay_in[r, h, :, i * UNIT:(i + 1) * UNIT]
                acc += res[rs, cols].astype(jnp.float32)
                hbuf[r, :, cols] = acc
                sq += acc * acc
        sq = jnp.sum(sq, axis=1, keepdims=True)
        packed = jnp.sum(jnp.where(eye, jnp.broadcast_to(sq, (RB, 128)), 0.0), axis=0, keepdims=True)
        sq_out[r] = packed
        sq_in[r, me] = packed
        hid[rs, :] = hbuf[r].astype(hid.dtype)
        for t in range(1, tp_size):
            pltpu.make_async_remote_copy(
                src_ref=sq_out.at[r], dst_ref=sq_in.at[r, me],
                send_sem=qsend_sem.at[0], recv_sem=qrecv_sem.at[r],
                device_id={"tp": lax.rem(me + t, tp_size)}, device_id_type=MESH).start()

        @pl.when(r >= LAG)
        def _():
            normalise(r - LAG)

    wait_bytes(rx, send_sem.at[0])
    wait_bytes(relay_out, rsend_sem.at[0])

    @pl.loop(chunks - LAG, chunks)
    def _(r):
        normalise(r)

    wait_bytes(sq_in.at[:, pl.ds(0, tp_size - 1)], qsend_sem.at[0])


def _write(hid, nrm, hid_hbm, nrm_hbm, sem):
    blocks = 4
    rows = hid.shape[0] // blocks
    copies = []
    for k, (src, dst) in enumerate(((hid, hid_hbm), (nrm, nrm_hbm))):
        for b in range(blocks):
            rs = pl.ds(b * rows, rows)
            copies.append(pltpu.make_async_copy(src.at[rs, :], dst.at[rs, :], sem.at[k, b]))
    for copy in copies:
        copy.start()
    for copy in copies:
        copy.wait()


def solution(mesh):
    tp_size = mesh.shape["tp"]

    def local_step(attn_blk, w_blk, resid_blk, gain_blk):
        rows, k_dim = attn_blk.shape
        d_local = resid_blk.shape[1]
        d_model = w_blk.shape[1]
        half = d_local // 2
        nu = half // UNIT
        units = tp_size * 2 * nu
        chunks = rows // RB
        assert tp_size == CORES * CHIPS and half % UNIT == 0 and rows % RB == 0
        hbm_spec = pl.BlockSpec(memory_space=pltpu.HBM)
        vmem_spec = pl.BlockSpec(memory_space=pltpu.VMEM)
        dma = pltpu.SemaphoreType.DMA
        out_shape = [jax.ShapeDtypeStruct((rows, d_local), jnp.bfloat16)] * 2
        hid, nrm = pl.pallas_call(
            functools.partial(_kernel, tp_size, d_model),
            out_shape=[pltpu.VMEM((rows, d_local), jnp.bfloat16)] * 2,
            in_specs=[hbm_spec] * 4,
            out_specs=[vmem_spec] * 2,
            scratch_shapes=[
                pltpu.VMEM((rows, k_dim), jnp.bfloat16),
                pltpu.VMEM((W_SLOTS, k_dim, UNIT), jnp.bfloat16),
                pltpu.VMEM((units, rows, UNIT), jnp.bfloat16),
                pltpu.VMEM((12 * nu, rows, UNIT), jnp.bfloat16),
                pltpu.VMEM((chunks, 2, RB, half), jnp.float32),
                pltpu.VMEM((chunks, 2, RB, half), jnp.float32),
                pltpu.VMEM((rows, d_local), jnp.bfloat16),
                pltpu.VMEM((d_local,), jnp.float32),
                pltpu.VMEM((chunks, RB, d_local), jnp.float32),
                pltpu.VMEM((chunks, 1, 128), jnp.float32),
                pltpu.VMEM((chunks, tp_size, 1, 128), jnp.float32),
                dma((A_BLOCKS,)),
                dma((2,)),
                dma((W_SLOTS,)),
                dma((1,)),
                dma((4,)),
                dma((1,)),
                dma((chunks,)),
                dma((1,)),
                dma((chunks,)),
            ],
            compiler_params=pltpu.CompilerParams(
                collective_id=0, has_side_effects=True, vmem_limit_bytes=62 * 1000 * 1000
            ),
            name="proj_scatter_norm",
        )(attn_blk, w_blk, resid_blk, gain_blk)
        return pl.pallas_call(
            _write,
            out_shape=out_shape,
            in_specs=[vmem_spec] * 2,
            out_specs=[hbm_spec] * 2,
            scratch_shapes=[dma((2, 4))],
            compiler_params=pltpu.CompilerParams(vmem_limit_bytes=8 * 1024 * 1024),
            name="write_out",
        )(hid, nrm)

    return jax.shard_map(
        local_step,
        mesh=mesh,
        in_specs=(P("data", "tp"), P("tp", None), P("data", "tp"), P("tp")),
        out_specs=(P("data", "tp"), P("data", "tp")),
        check_vma=False,
    )
```

time: 122 us -> 115 us (0.943)
  local copies, waits for them, and re-layouts: 5.21 us -> 0 us
  Pallas kernels: 116 us -> 114 us
    unnamed x4 -> x0, local copies, waits for them, and re-layouts: 3.92 us -> none
    pallas_call x1 -> x2, Pallas kernels: 116 us -> 114 us  [the longest x1 112 us: local_step(): pl.pallas_call(functools.partial(_kernel, tp_size, d_model), out_shape=[p...]
    reshape x1 -> x0, local copies, waits for them, and re-layouts: 1.3 us -> none  [local_step(): gain_blk.reshape(1, d_local)]
where the time goes in v2:
time: 115 us
  Pallas kernels  114 us (99%)
    pallas_call x1, Pallas kernels, local_step(): pl.pallas_call(functools.partial(_kernel, tp_size, d_model), out_shape=[p...  112 us

profile of v2, /device:TPU:113, one launch (start us, length us, event | category | flops | bytes accessed | tf_op | source)
XLA Modules:
  0.0 114.6 jit_solution(11233169814274029376)
XLA Ops:
  0.6 112.3 %proj_scatter_norm.1 = (bf16[512,1536]{1,0:T(8,128)(2,1)S(1)}, bf16[512,1536]{1,0:T(8,128)(2,1)S(1)}) custom-call(bf16[512,1536]{1,0:T(8,128)(2,1)} %a_hbm.1, bf16[1536,12288]{1,0:T(8,128)(2,1)} %w_hbm.1, bf16[512,1536]{1,0:T(8,128)(2,1)} %r_hbm.1, f32[1536]{0:T(1024)} %g_hbm.1), custom_call_target="tpu_custom_call" | custom-call | tf_op jit(solution)/shard_map/proj_scatter_norm/pallas_call | solution.py:240
  112.9 1.7 %write_out.1 = (bf16[512,1536]{1,0:T(8,128)(2,1)}, bf16[512,1536]{1,0:T(8,128)(2,1)}) custom-call(bf16[512,1536]{1,0:T(8,128)(2,1)S(1)} %get-tuple-element.4.hid, bf16[512,1536]{1,0:T(8,128)(2,1)S(1)} %get-tuple-element.5.nrm), custom_call_target="tpu_custom_call" | custom-call | tf_op jit(solution)/shard_map/write_out/pallas_call | solution.py:272

commit v3 on v2

--- a/solution.py
+++ b/solution.py
@@ -15,7 +15,6 @@
 W_SLOTS = 4
 RB = 64
 AHEAD = 3
-LAG = 3
 A_BLOCKS = 4
 
 
@@ -79,30 +78,34 @@
     def chunk_rows(r):
         return pl.ds(pl.multiple_of(r * RB, RB), RB)
 
+    w_copy(jnp.int32(0)).start()
+    a_copy(0).start()
+
+    peers = [x * CORES + 1 - c] + [chip(o, core) for o in (1, CHIPS - 1) for core in range(CORES)]
     barrier = pltpu.get_barrier_semaphore()
-    for t in range(1, tp_size):
-        pl.semaphore_signal(barrier, inc=1, device_id={"tp": lax.rem(me + t, tp_size)}, device_id_type=MESH)
-
-    w_copy(jnp.int32(0)).start()
-    for b in range(A_BLOCKS):
+    for peer in peers:
+        pl.semaphore_signal(barrier, inc=1, device_id={"tp": peer}, device_id_type=MESH)
+
+    for b in range(1, A_BLOCKS):
         a_copy(b).start()
-    for s in range(1, W_SLOTS):
-        w_copy(jnp.int32(s)).start()
     r_copy = pltpu.make_async_copy(r_hbm, res, in_sem.at[0])
-    r_copy.start()
     g_copy = pltpu.make_async_copy(g_hbm, gain, in_sem.at[1])
-    g_copy.start()
 
     _, i0, _, e0, h0 = decode(jnp.int32(0))
     w_copy(jnp.int32(0)).wait()
     for b in range(A_BLOCKS):
         a_copy(b).wait()
+        if b == 0:
+            for s in range(1, W_SLOTS):
+                w_copy(jnp.int32(s)).start()
         rs = pl.ds(b * ab, ab)
         p[0, rs, :] = jnp.dot(a[rs, :], w[0], preferred_element_type=jnp.float32).astype(p.dtype)
         if b == 0:
-            pl.semaphore_wait(barrier, tp_size - 1)
+            pl.semaphore_wait(barrier, len(peers))
         send_rows(0, (h0 * 2 + c) * nu + i0, 0, chip(3 + 2 * h0, e0), rs)
     w_copy(jnp.int32(W_SLOTS)).start()
+    r_copy.start()
+    g_copy.start()
 
     @pl.loop(1, total)
     def _(s):
@@ -153,58 +156,83 @@
     eye = (lax.broadcasted_iota(jnp.int32, (RB, 128), 0)
            == lax.broadcasted_iota(jnp.int32, (RB, 128), 1))
 
+    def columns():
+        for h in range(2):
+            for i in range(nu):
+                yield h, i, slice(h * half + i * UNIT, h * half + (i + 1) * UNIT)
+
+    def add_early(r):
+        rs = chunk_rows(r)
+        for h, i, cols in columns():
+            acc = p[local_unit(2, h, i), rs, :].astype(jnp.float32)
+            acc += rx[(8 + h) * nu + i, rs, :].astype(jnp.float32)
+            acc += rx[(4 + h * 2) * nu + i, rs, :].astype(jnp.float32)
+            acc += rx[(5 + h * 2) * nu + i, rs, :].astype(jnp.float32)
+            hbuf[r, :, cols] = acc + res[rs, cols].astype(jnp.float32)
+
+    def finish(r):
+        sq = jnp.zeros((RB, UNIT), jnp.float32)
+        for h, i, cols in columns():
+            acc = hbuf[r, :, cols] + relay_in[r, h, :, i * UNIT:(i + 1) * UNIT]
+            hbuf[r, :, cols] = acc
+            sq += acc * acc
+        sq = jnp.sum(sq, axis=1, keepdims=True)
+        packed = jnp.sum(jnp.where(eye, jnp.broadcast_to(sq, (RB, 128)), 0.0), axis=0, keepdims=True)
+        sq_out[r] = packed
+        sq_in[me, r] = packed
+
+    def send_sums(lo, n, k):
+        for t in range(1, tp_size):
+            pltpu.make_async_remote_copy(
+                src_ref=sq_out.at[pl.ds(lo, n)], dst_ref=sq_in.at[me, pl.ds(lo, n)],
+                send_sem=qsend_sem.at[k], recv_sem=qrecv_sem.at[k],
+                device_id={"tp": lax.rem(me + t, tp_size)}, device_id_type=MESH).start()
+
+    def wait_sums(lo, n, sem):
+        wait_bytes(sq_in.at[pl.ds(0, tp_size - 1), pl.ds(lo, n)], sem)
+
     def normalise(r):
-        wait_bytes(sq_in.at[r, pl.ds(0, tp_size - 1)], qrecv_sem.at[r])
-        tot = sq_in[r, 0]
+        tot = sq_in[0, r]
         for t in range(1, tp_size):
-            tot += sq_in[r, t]
+            tot += sq_in[t, r]
         col = jnp.sum(jnp.where(eye, jnp.broadcast_to(tot, (RB, 128)), 0.0), axis=1, keepdims=True)
         scale = lax.rsqrt(col / d_model + EPS)
         nrm[chunk_rows(r), :] = (hbuf[r] * scale * gain[...].reshape(1, d_local)).astype(nrm.dtype)
 
-    @pl.loop(0, chunks)
+    def write_hidden(r):
+        hid[chunk_rows(r), :] = hbuf[r].astype(hid.dtype)
+
+    last = chunks - 1
+
+    @pl.loop(0, last)
     def _(r):
         @pl.when(r + AHEAD < chunks)
         def _():
             send_relay(r + AHEAD)
 
+        add_early(r)
         wait_bytes(relay_in.at[r], rrecv_sem.at[r])
-        rs = chunk_rows(r)
-        sq = jnp.zeros((RB, UNIT), jnp.float32)
-        for h in range(2):
-            for i in range(nu):
-                cols = slice(h * half + i * UNIT, h * half + (i + 1) * UNIT)
-                acc = p[local_unit(2, h, i), rs, :].astype(jnp.float32)
-                acc += rx[(8 + h) * nu + i, rs, :].astype(jnp.float32)
-                acc += rx[(4 + h * 2) * nu + i, rs, :].astype(jnp.float32)
-                acc += rx[(5 + h * 2) * nu + i, rs, :].astype(jnp.float32)
-                acc += relay_in[r, h, :, i * UNIT:(i + 1) * UNIT]
-                acc += res[rs, cols].astype(jnp.float32)
-                hbuf[r, :, cols] = acc
-                sq += acc * acc
-        sq = jnp.sum(sq, axis=1, keepdims=True)
-        packed = jnp.sum(jnp.where(eye, jnp.broadcast_to(sq, (RB, 128)), 0.0), axis=0, keepdims=True)
-        sq_out[r] = packed
-        sq_in[r, me] = packed
-        hid[rs, :] = hbuf[r].astype(hid.dtype)
-        for t in range(1, tp_size):
-            pltpu.make_async_remote_copy(
-                src_ref=sq_out.at[r], dst_ref=sq_in.at[r, me],
-                send_sem=qsend_sem.at[0], recv_sem=qrecv_sem.at[r],
-                device_id={"tp": lax.rem(me + t, tp_size)}, device_id_type=MESH).start()
-
-        @pl.when(r >= LAG)
-        def _():
-            normalise(r - LAG)
-
+        finish(r)
+        write_hidden(r)
+
+    send_sums(0, last, 0)
+    add_early(last)
     wait_bytes(rx, send_sem.at[0])
-    wait_bytes(relay_out, rsend_sem.at[0])
-
-    @pl.loop(chunks - LAG, chunks)
+    wait_sums(0, last, qrecv_sem.at[0])
+
+    @pl.loop(0, last)
     def _(r):
         normalise(r)
 
-    wait_bytes(sq_in.at[:, pl.ds(0, tp_size - 1)], qsend_sem.at[0])
+    wait_bytes(relay_in.at[last], rrecv_sem.at[last])
+    finish(last)
+    send_sums(last, 1, 1)
+    write_hidden(last)
+    wait_bytes(relay_out, rsend_sem.at[0])
+    wait_sums(0, last, qsend_sem.at[0])
+    wait_sums(last, 1, qrecv_sem.at[1])
+    normalise(last)
+    wait_sums(last, 1, qsend_sem.at[1])
 
 
 def _write(hid, nrm, hid_hbm, nrm_hbm, sem):
@@ -253,7 +281,7 @@
                 pltpu.VMEM((d_local,), jnp.float32),
                 pltpu.VMEM((chunks, RB, d_local), jnp.float32),
                 pltpu.VMEM((chunks, 1, 128), jnp.float32),
-                pltpu.VMEM((chunks, tp_size, 1, 128), jnp.float32),
+                pltpu.VMEM((tp_size, chunks, 1, 128), jnp.float32),
                 dma((A_BLOCKS,)),
                 dma((2,)),
                 dma((W_SLOTS,)),
@@ -261,8 +289,8 @@
                 dma((4,)),
                 dma((1,)),
                 dma((chunks,)),
-                dma((1,)),
-                dma((chunks,)),
+                dma((2,)),
+                dma((2,)),
             ],
             compiler_params=pltpu.CompilerParams(
                 collective_id=0, has_side_effects=True, vmem_limit_bytes=62 * 1000 * 1000

time: 115 us -> 116 us (level)
    pallas_call x1, Pallas kernels: 112 us -> 114 us  [local_step(): pl.pallas_call(functools.partial(_kernel, tp_size, d_model), out_shape=[p...]
where the time goes in v3:
time: 116 us
  Pallas kernels  115 us (99%)
    pallas_call x1, Pallas kernels, local_step(): pl.pallas_call(functools.partial(_kernel, tp_size, d_model), out_shape=[p...  114 us

profile of v3, /device:TPU:113, one launch (start us, length us, event | category | flops | bytes accessed | tf_op | source)
XLA Modules:
  0.0 116.1 jit_solution(1397911010778585065)
XLA Ops:
  0.6 113.7 %proj_scatter_norm.1 = (bf16[512,1536]{1,0:T(8,128)(2,1)S(1)}, bf16[512,1536]{1,0:T(8,128)(2,1)S(1)}) custom-call(bf16[512,1536]{1,0:T(8,128)(2,1)} %a_hbm.1, bf16[1536,12288]{1,0:T(8,128)(2,1)} %w_hbm.1, bf16[512,1536]{1,0:T(8,128)(2,1)} %r_hbm.1, f32[1536]{0:T(1024)} %g_hbm.1), custom_call_target="tpu_custom_call" | custom-call | tf_op jit(solution)/shard_map/proj_scatter_norm/pallas_call | solution.py:268
  114.4 1.7 %write_out.1 = (bf16[512,1536]{1,0:T(8,128)(2,1)}, bf16[512,1536]{1,0:T(8,128)(2,1)}) custom-call(bf16[512,1536]{1,0:T(8,128)(2,1)S(1)} %get-tuple-element.4.hid, bf16[512,1536]{1,0:T(8,128)(2,1)S(1)} %get-tuple-element.5.nrm), custom_call_target="tpu_custom_call" | custom-call | tf_op jit(solution)/shard_map/write_out/pallas_call | solution.py:300

commit v4 on v3

--- a/solution.py
+++ b/solution.py
@@ -218,18 +218,18 @@
     send_sums(0, last, 0)
     add_early(last)
     wait_bytes(rx, send_sem.at[0])
-    wait_sums(0, last, qrecv_sem.at[0])
-
-    @pl.loop(0, last)
-    def _(r):
-        normalise(r)
-
     wait_bytes(relay_in.at[last], rrecv_sem.at[last])
     finish(last)
     send_sums(last, 1, 1)
     write_hidden(last)
     wait_bytes(relay_out, rsend_sem.at[0])
     wait_sums(0, last, qsend_sem.at[0])
+    wait_sums(0, last, qrecv_sem.at[0])
+
+    @pl.loop(0, last)
+    def _(r):
+        normalise(r)
+
     wait_sums(last, 1, qrecv_sem.at[1])
     normalise(last)
     wait_sums(last, 1, qsend_sem.at[1])

time: 116 us -> 114 us (0.983)
  Pallas kernels: 115 us -> 113 us
    pallas_call x1, Pallas kernels: 114 us -> 111 us  [local_step(): pl.pallas_call(functools.partial(_kernel, tp_size, d_model), out_shape=[p...]
where the time goes in v4:
time: 114 us
  Pallas kernels  113 us (99%)
    pallas_call x1, Pallas kernels, local_step(): pl.pallas_call(functools.partial(_kernel, tp_size, d_model), out_shape=[p...  111 us

profile of v4, /device:TPU:113, one launch (start us, length us, event | category | flops | bytes accessed | tf_op | source)
XLA Modules:
  0.0 113.7 jit_solution(1777133913646537672)
XLA Ops:
  0.6 111.3 %proj_scatter_norm.1 = (bf16[512,1536]{1,0:T(8,128)(2,1)S(1)}, bf16[512,1536]{1,0:T(8,128)(2,1)S(1)}) custom-call(bf16[512,1536]{1,0:T(8,128)(2,1)} %a_hbm.1, bf16[1536,12288]{1,0:T(8,128)(2,1)} %w_hbm.1, bf16[512,1536]{1,0:T(8,128)(2,1)} %r_hbm.1, f32[1536]{0:T(1024)} %g_hbm.1), custom_call_target="tpu_custom_call" | custom-call | tf_op jit(solution)/shard_map/proj_scatter_norm/pallas_call | solution.py:268
  112.0 1.7 %write_out.1 = (bf16[512,1536]{1,0:T(8,128)(2,1)}, bf16[512,1536]{1,0:T(8,128)(2,1)}) custom-call(bf16[512,1536]{1,0:T(8,128)(2,1)S(1)} %get-tuple-element.4.hid, bf16[512,1536]{1,0:T(8,128)(2,1)S(1)} %get-tuple-element.5.nrm), custom_call_target="tpu_custom_call" | custom-call | tf_op jit(solution)/shard_map/write_out/pallas_call | solution.py:300

commit v5 on v4

--- a/solution.py
+++ b/solution.py
@@ -13,8 +13,8 @@
 CHIPS = 4
 UNIT = 256
 W_SLOTS = 4
-RB = 64
-AHEAD = 3
+RB = 32
+AHEAD = 6
 A_BLOCKS = 4
 
 

time: 114 us -> 115 us (level)
  no operation moved by 1% of the time
where the time goes in v5:
time: 115 us
  Pallas kernels  114 us (99%)
    pallas_call x1, Pallas kernels, local_step(): pl.pallas_call(functools.partial(_kernel, tp_size, d_model), out_shape=[p...  112 us

profile of v5, /device:TPU:113, one launch (start us, length us, event | category | flops | bytes accessed | tf_op | source)
XLA Modules:
  0.0 114.7 jit_solution(7943243189850440804)
XLA Ops:
  0.6 112.4 %proj_scatter_norm.1 = (bf16[512,1536]{1,0:T(8,128)(2,1)S(1)}, bf16[512,1536]{1,0:T(8,128)(2,1)S(1)}) custom-call(bf16[512,1536]{1,0:T(8,128)(2,1)} %a_hbm.1, bf16[1536,12288]{1,0:T(8,128)(2,1)} %w_hbm.1, bf16[512,1536]{1,0:T(8,128)(2,1)} %r_hbm.1, f32[1536]{0:T(1024)} %g_hbm.1), custom_call_target="tpu_custom_call" | custom-call | tf_op jit(solution)/shard_map/proj_scatter_norm/pallas_call | solution.py:268
  113.0 1.7 %write_out.1 = (bf16[512,1536]{1,0:T(8,128)(2,1)}, bf16[512,1536]{1,0:T(8,128)(2,1)}) custom-call(bf16[512,1536]{1,0:T(8,128)(2,1)S(1)} %get-tuple-element.4.hid, bf16[512,1536]{1,0:T(8,128)(2,1)S(1)} %get-tuple-element.5.nrm), custom_call_target="tpu_custom_call" | custom-call | tf_op jit(solution)/shard_map/write_out/pallas_call | solution.py:300
